TPU v7x, 32 devices: a whole 2x2x4 slice. The times are simulated.
32 devices in a mesh: req: 2 (over y), patch: 16 (over z, x, core).
Axes of the slice: x: 2, y: 2, z: 4, core: 2. Of those that a mesh axis runs over, the one named last changes fastest.
Arguments:
- tokens: bfloat16 [1536, 1152], P(('req', 'patch')), parts along dimension 0, may hold values from -6 to 6
- positions: int32 [2, 1536], P(None, ('req', 'patch')), parts along dimension 1, may hold values from 0 to 95
- counts: int32 [32], P('req'), parts along dimension 0, may hold values from 1 to 48, 384 in all
- timestep: int32 [2], P('req'), parts along dimension 0, may hold values from 0 to 999
- time_in: bfloat16 [256, 1152], replicated, may hold values from -0.375 to 0.375
- time_out: bfloat16 [1152, 1152], P(None, 'patch'), may hold values from -0.1875 to 0.1875
- ada_weight: bfloat16 [1152, 3456], P('patch'), may hold values from -0.375 to 0.375
- qkv_weight: bfloat16 [1152, 3456], replicated, may hold values from -2 to 2, as said below
- out_weight: bfloat16 [1152, 1152], replicated, may hold values from -0.1875 to 0.1875
Outputs:
- block_out: bfloat16 [1536, 1152], P(('req', 'patch')), parts along dimension 0
There are 2 independent parts, one for each index of `req`. A program takes and returns all parts, laid end to end along the dimension named above; an argument that names none is the same for every part. Nothing has to cross between parts.
Inputs may be any that keep to these rules, and one draw needn't show every extreme that they name: `counts`: used slots are the first ones of each block; they sum to exactly 384, and some block uses all 48. `qkv_weight`: columns are 1152 of queries, 1152 of keys, 1152 of values, each head's 72 columns side by side.
All inputs are finite; a program needn't handle non-finite values.
Results may differ from a plain program's by a relative error of at most 0.0039.
Values may be sent and summed in bfloat16 or wider, within the bound.
No kernel may reach another device: no remote copies, remote signals or barrier semaphores. Data moves between devices by JAX's collectives and lax.ppermute only.
A program may use at most 64 MiB of HBM per device.

v0:
```python
import math

import jax
import jax.numpy as jnp
from jax import lax
from jax.sharding import PartitionSpec as P

HEADS = 16


neg_large = -1e30
key_block = 512


def time_features(timestep, freq_size):
    half_size = freq_size // 2
    frequencies = jnp.exp(-math.log(10000.0) * jnp.arange(half_size, dtype=jnp.float32) / half_size)
    angles = timestep.astype(jnp.float32)[:, None] * frequencies[None, :]
    return jnp.concatenate([jnp.cos(angles), jnp.sin(angles)], axis=1).astype(jnp.bfloat16)


def position_table(positions, model_width):
    quarter = model_width // 4
    omegas = jnp.power(10000.0, -jnp.arange(quarter, dtype=jnp.float32) / quarter)
    row_angle = positions[0].astype(jnp.float32)[:, None] * omegas[None, :]
    col_angle = positions[1].astype(jnp.float32)[:, None] * omegas[None, :]
    return jnp.concatenate(
        [jnp.sin(row_angle), jnp.cos(row_angle), jnp.sin(col_angle), jnp.cos(col_angle)], axis=1
    )


def attend_update(running, query_heads, key_piece, value_piece, mask_piece, inv_root):
    row_top, denominator, weighted = running
    key_count = key_piece.shape[0]
    head_count = query_heads.shape[1]
    head_size = query_heads.shape[2]
    key_heads = key_piece.reshape(key_count, head_count, head_size)
    value_heads = value_piece.reshape(key_count, head_count, head_size)
    scores = (
        jnp.einsum("qhd,khd->hqk", query_heads, key_heads, preferred_element_type=jnp.float32)
        * inv_root
    )
    scores = jnp.where(mask_piece[None, None, :], scores, neg_large)
    new_top = jnp.maximum(row_top, jnp.max(scores, axis=2))
    weights = jnp.where(mask_piece[None, None, :], jnp.exp(scores - new_top[:, :, None]), 0.0)
    factor = jnp.exp(row_top - new_top)
    denominator = denominator * factor + jnp.sum(weights, axis=2)
    rounded = weights.astype(jnp.bfloat16)
    weighted = weighted * factor[:, :, None] + jnp.einsum(
        "hqk,khd->hqd", rounded, value_heads, preferred_element_type=jnp.float32
    )
    return (new_top, denominator, weighted)


def make_folder(query_heads, key_valid, inv_root):

    def fold_keys(running, shard_piece, start_row):
        key_piece, value_piece = shard_piece
        key_count = key_piece.shape[0]
        if key_count > 2 * key_block and key_count % key_block == 0:
            block_total = key_count // key_block

            def block_step(carried, block_items):
                return (
                    attend_update(
                        carried,
                        query_heads,
                        block_items[0],
                        block_items[1],
                        block_items[2],
                        inv_root,
                    ),
                    None,
                )

            stacked = (
                key_piece.reshape(block_total, key_block, key_piece.shape[1]),
                value_piece.reshape(block_total, key_block, value_piece.shape[1]),
                key_valid.reshape(block_total, key_block),
            )
            running, unused = lax.scan(block_step, running, stacked)
            return running
        return attend_update(running, query_heads, key_piece, value_piece, key_valid, inv_root)

    return fold_keys


def initial_state(query_rows, head_count, head_size):
    return (
        jnp.full((head_count, query_rows), neg_large, jnp.float32),
        jnp.zeros((head_count, query_rows), jnp.float32),
        jnp.zeros((head_count, query_rows, head_size), jnp.float32),
    )


def finish_state(running):
    row_top, denominator, weighted = running
    normalized = weighted / denominator[:, :, None]
    head_count, query_rows, head_size = normalized.shape
    return (
        jnp.transpose(normalized, (1, 0, 2))
        .reshape(query_rows, head_count * head_size)
        .astype(jnp.bfloat16)
    )


def per_device(
    tokens, positions, counts, timestep, time_in, time_out, ada_weight, qkv_weight, out_weight
):
    devices = lax.axis_size("patch")
    my_index = lax.axis_index("patch")
    local_rows = tokens.shape[0]
    model_width = tokens.shape[1]
    head_count = HEADS
    head_size = model_width // head_count
    inv_root = 1.0 / math.sqrt(head_size)
    features = time_features(timestep, time_in.shape[0])
    hidden_time = jax.nn.silu(
        jnp.dot(features, time_in, preferred_element_type=jnp.float32)
    ).astype(jnp.bfloat16)
    cond_part = jnp.dot(hidden_time, time_out, preferred_element_type=jnp.float32)
    activated = jax.nn.silu(cond_part).astype(jnp.bfloat16)
    partial_mod = jnp.dot(activated, ada_weight, preferred_element_type=jnp.float32)
    modulation = lax.psum(partial_mod, "patch")
    shift_mod = modulation[:, :model_width]
    scale_mod = modulation[:, model_width : 2 * model_width]
    gate_mod = modulation[:, 2 * model_width :]
    x_in = tokens.astype(jnp.float32) + position_table(positions, model_width)
    mean_value = jnp.mean(x_in, axis=1, keepdims=True)
    centered = x_in - mean_value
    variance = jnp.mean(centered * centered, axis=1, keepdims=True)
    normed = centered * lax.rsqrt(variance + 1e-06)
    modulated = (normed * (1.0 + scale_mod) + shift_mod).astype(jnp.bfloat16)
    counts_here = lax.dynamic_index_in_dim(counts, my_index, keepdims=False)
    row_ids = jnp.arange(local_rows, dtype=jnp.int32)
    row_valid = row_ids < counts_here
    projections = jnp.dot(modulated, qkv_weight, preferred_element_type=jnp.float32).astype(
        jnp.bfloat16
    )
    groups = devices // head_count
    part_rows = local_rows // groups
    query_split = projections[:, :model_width].reshape(groups, part_rows, head_count, head_size)
    query_send = jnp.transpose(query_split, (0, 2, 1, 3)).reshape(devices, part_rows, head_size)
    key_split = projections[:, model_width : 2 * model_width].reshape(
        local_rows, head_count, head_size
    )
    value_split = projections[:, 2 * model_width :].reshape(local_rows, head_count, head_size)
    pair_heads = jnp.transpose(jnp.concatenate([key_split, value_split], axis=2), (1, 0, 2))
    pair_send = jnp.broadcast_to(pair_heads[None], (groups, head_count, local_rows, 2 * head_size))
    pair_send = pair_send.reshape(devices, local_rows, 2 * head_size)
    got_query, got_pair = (
        lax.all_to_all(query_send, "patch", split_axis=0, concat_axis=0, tiled=True),
        lax.all_to_all(pair_send, "patch", split_axis=0, concat_axis=0, tiled=True),
    )
    query_rows = devices * part_rows
    query_heads = got_query.reshape(query_rows, 1, head_size)
    all_pairs = got_pair.reshape(devices * local_rows, 2 * head_size)
    key_valid = (jnp.arange(local_rows, dtype=jnp.int32)[None, :] < counts[:, None]).reshape(-1)
    folder = make_folder(query_heads, key_valid, inv_root)
    running = folder(
        initial_state(query_rows, 1, head_size),
        (all_pairs[:, :head_size], all_pairs[:, head_size:]),
        0,
    )
    head_result = finish_state(running).reshape(devices, part_rows, head_size)
    came_back = lax.all_to_all(head_result, "patch", split_axis=0, concat_axis=0, tiled=True)
    attended = jnp.transpose(
        came_back.reshape(groups, head_count, part_rows, head_size), (0, 2, 1, 3)
    )
    attended = attended.reshape(local_rows, model_width)
    projected = jnp.dot(attended, out_weight, preferred_element_type=jnp.float32)
    valid_column = row_valid.astype(jnp.float32)[:, None]
    return (x_in + gate_mod * projected * valid_column).astype(jnp.bfloat16)


def solution(mesh):
    placed = (
        P(("req", "patch"), None),
        P(None, ("req", "patch")),
        P("req"),
        P("req"),
        P(),
        P(None, "patch"),
        P("patch", None),
        P(),
        P(),
    )
    return jax.shard_map(
        per_device, mesh=mesh, in_specs=placed, out_specs=P(("req", "patch"), None), check_vma=False
    )
```

profile of v0, /device:TPU:0, one launch (start us, length us, event | category | flops | bytes accessed | tf_op | source)
XLA Modules:
  0.0 123.4 jit_solution(13335369351316423858)
XLA Ops:
  0.0 0.9 convert_bitcast_fusion
  0.9 0.6 multiply_cosine_fusion
  1.5 0.1 concatenate.13
  1.6 1.0 fusion.25
  2.7 1.1 multiply_reduce_fusion
  4.5 1.3 %convolution_reduce_fusion = f32[1152]{0:T(1024)S(1)} fusion(bf16[256,1]{0,1:T(2,128)(2,1)S(1)} %reshape.180, bf16[256,1152]{1,0:T(8,128)(2,1)} %param.13), kind=kOutput, calls=%fused_computation.15 | convolution fusion | flops 589824 | bytes 594944 | tf_op jit(solution)/shard_map/dot_general | solution.py:119
  5.8 1.6 %fusion.27 = f32[1,3456]{1,0:T(1,128)S(1)} fusion(bf16[72,3456]{1,0:T(8,128)(2,1)} %param.15, bf16[1152,1]{0,1:T(2,128)(2,1)S(1)} %reshape.182, bf16[1152,72]{0,1:T(8,128)(2,1)} %param.14), kind=kOutput, calls=%fused_computation.46 | convolution fusion | flops 663912 | bytes 679680 | tf_op jit(solution)/shard_map/dot_general | solution.py:123
  7.4 63.0 %psum.7 = f32[1,3456]{1,0:T(1,128)S(1)} all-reduce(f32[1,3456]{1,0:T(1,128)S(1)} %fusion.27), channel_id=1, replica_groups=mesh['req'=2,'patch'=16] {'patch'}, use_global_device_ids=true, to_apply=%region_0.1 | all-reduce | flops 3456 | bytes 27648 | tf_op jit(solution)/shard_map/psum | solution.py:124
  70.4 4.6 %convolution_convert_fusion = bf16[48,3456]{1,0:T(8,128)(2,1)S(1)} fusion(bf16[1152,3456]{1,0:T(8,128)(2,1)} %param.16, f32[1152]{0:T(1024)S(1)} %get-tuple-element.6, f32[1152]{0:T(1024)S(1)} %get-tuple-element.7, f32[48]{0:T(128)S(1)} %add_rsqrt_fusion, f32[48]{0:T(128)S(1)} %broadcast_multiply_fusion, f32[48,1152]{1,0:T(8,128)S(1)} %concatenate.13, ...), kind=kOutput, calls=%fused_computation | convolution fusion | flops 382758912 | bytes 8635776 | tf_op jit(solution)/shard_map/dot_general | solution.py:137
  75.0 0.7 fusion.38
  75.7 0.3 reshape.172
  76.1 0.7 copy.16
  76.8 3.5 %all-to-all-start = ((bf16[16,48,72]{2,1,0:T(8,128)(2,1)}), bf16[16,48,72]{2,1,0:T(8,128)(2,1)S(1)}, u32[]{:S(2)}, u32[]{:S(2)}) async-start(bf16[16,48,72]{2,1,0:T(8,128)(2,1)} %bitcast.38), calls=%async_computation | async-start | bytes 393216 | tf_op jit(solution)/shard_map/all_to_all | solution.py:152
  80.3 1.2 %reshape.175 = bf16[48,16,72]{2,1,0:T(8,128)(2,1)S(1)} reshape(bf16[48,1152]{1,0:T(8,128)(2,1)} %get-tuple-element.8) | data formatting | bytes 221184 | tf_op jit(solution)/shard_map/reshape | solution.py:144
  81.6 0.7 copy.11
  82.3 0.3 reshape.176
  82.7 1.8 %maximum_bitcast_fusion = bf16[16,48,144]{2,1,0:T(8,128)(2,1)} fusion(bf16[48,16,72]{2,0,1:T(8,128)(2,1)S(1)} %copy.12, bf16[48,16,72]{2,0,1:T(8,128)(2,1)} %copy.11), kind=kLoop, calls=%fused_computation.17 | loop fusion | flops 442368 | bytes 442368 | tf_op jit(solution)/shard_map/transpose | solution.py:148
  84.5 4.7 %all-to-all-done = bf16[16,48,72]{2,1,0:T(8,128)(2,1)S(1)} async-done(((bf16[16,48,72]{2,1,0:T(8,128)(2,1)}), bf16[16,48,72]{2,1,0:T(8,128)(2,1)S(1)}, u32[]{:S(2)}, u32[]{:S(2)}) %all-to-all-start) | async-done | bytes 110624 | tf_op jit(solution)/shard_map/all_to_all | solution.py:152
  89.2 0.7 copy-done.2
  89.9 3.6 %all-to-all-start.1 = ((bf16[16,48,144]{2,1,0:T(8,128)(2,1)}), bf16[16,48,144]{2,1,0:T(8,128)(2,1)S(1)}, u32[]{:S(2)}, u32[]{:S(2)}) async-start(bf16[16,48,144]{2,1,0:T(8,128)(2,1)} %maximum_bitcast_fusion), calls=%async_computation.1 | async-start | bytes 786432 | tf_op jit(solution)/shard_map/all_to_all | solution.py:153
  93.6 0.1 lt.37
  93.6 12.0 %all-to-all-done.1 = bf16[16,48,144]{2,1,0:T(8,128)(2,1)S(1)} async-done(((bf16[16,48,144]{2,1,0:T(8,128)(2,1)}), bf16[16,48,144]{2,1,0:T(8,128)(2,1)S(1)}, u32[]{:S(2)}, u32[]{:S(2)}) %all-to-all-start.1) | async-done | bytes 221216 | tf_op jit(solution)/shard_map/all_to_all | solution.py:153
  105.6 1.5 %fusion.3 = (f32[768]{0:T(1024)S(1)}, f32[768,768]{0,1:T(8,128)S(1)}) fusion(pred[768]{0:T(1024)(128)(4,1)S(1)} %lt.37, bf16[768,72]{1,0:T(8,128)(2,1)} %bitcast.41, bf16[768,144]{1,0:T(8,128)(2,1)S(1)} %bitcast.39), kind=kOutput, calls=%fused_computation.7 | convolution fusion | flops 86703360 | bytes 2670592 | tf_op jit(solution)/shard_map/qhd,khd->hqk/dot_general | solution.py:40
  107.1 0.6 fusion.4
  107.7 0.8 fusion.15
  108.6 0.8 copy.13
  109.4 3.5 %all-to-all-start.2 = ((bf16[16,48,72]{2,1,0:T(8,128)(2,1)}), bf16[16,48,72]{2,1,0:T(8,128)(2,1)S(1)}, u32[]{:S(2)}, u32[]{:S(2)}) async-start(bf16[16,48,72]{2,1,0:T(8,128)(2,1)} %bitcast.10), calls=%async_computation.2 | async-start | bytes 393216 | tf_op jit(solution)/shard_map/all_to_all | solution.py:166
  112.9 0.6 dynamic_slice.4
  113.5 0.6 compare_convert_fusion
  114.1 7.7 %all-to-all-done.2 = bf16[16,48,72]{2,1,0:T(8,128)(2,1)S(1)} async-done(((bf16[16,48,72]{2,1,0:T(8,128)(2,1)}), bf16[16,48,72]{2,1,0:T(8,128)(2,1)S(1)}, u32[]{:S(2)}, u32[]{:S(2)}) %all-to-all-start.2) | async-done | bytes 110624 | tf_op jit(solution)/shard_map/all_to_all | solution.py:166
  121.9 0.2 reshape.179
  122.1 1.2 %fusion.2 = bf16[48,1152]{1,0:T(8,128)(2,1)} fusion(bf16[48,1152]{1,0:T(8,128)(2,1)S(1)} %reshape.179, bf16[1152,1152]{1,0:T(8,128)(2,1)S(1)} %copy-done, f32[48]{0:T(128)S(1)} %compare_convert_fusion, f32[1152]{0:T(1024)S(1)} %get-tuple-element.5, f32[48,1152]{1,0:T(8,128)S(1)} %concatenate.13, bf16[48,1152]{1,0:T(8,128)(2,1)S(1)} %copy-done.1), kind=kOutput, calls=%fused_computation.6 | convolution fusion | flops 127733760 | bytes 3211968 | tf_op jit(solution)/shard_map/dot_general | solution.py:171
  (21 shorter events, 0.4 us)
Async XLA Ops:
  0.0 122.1 %copy-start = (bf16[1152,1152]{1,0:T(8,128)(2,1)S(1)}, bf16[1152,1152]{1,0:T(8,128)(2,1)}, u32[]{:S(2)}) copy-start(bf16[1152,1152]{1,0:T(8,128)(2,1)} %param.17) | copy-start | bytes 7962628
  0.0 70.4 %copy-start.1 = (bf16[48,1152]{1,0:T(8,128)(2,1)S(1)}, bf16[48,1152]{1,0:T(8,128)(2,1)}, u32[]{:S(2)}) copy-start(bf16[48,1152]{1,0:T(8,128)(2,1)} %param.9) | copy-start | bytes 331780
  75.0 18.4 %copy-start.3 = (s32[16]{0:T(128)S(1)}, s32[16]{0:T(128)}, u32[]{:S(2)}) copy-start(s32[16]{0:T(128)} %param.11) | copy-start | bytes 196
  76.8 12.5 %all-to-all-start = ((bf16[16,48,72]{2,1,0:T(8,128)(2,1)}), bf16[16,48,72]{2,1,0:T(8,128)(2,1)S(1)}, u32[]{:S(2)}, u32[]{:S(2)}) async-start(bf16[16,48,72]{2,1,0:T(8,128)(2,1)} %bitcast.38), calls=%async_computation | async-start | bytes 393216 | tf_op jit(solution)/shard_map/all_to_all | solution.py:152
  89.2 0.7 copy-start.2
  89.9 15.7 %all-to-all-start.1 = ((bf16[16,48,144]{2,1,0:T(8,128)(2,1)}), bf16[16,48,144]{2,1,0:T(8,128)(2,1)S(1)}, u32[]{:S(2)}, u32[]{:S(2)}) async-start(bf16[16,48,144]{2,1,0:T(8,128)(2,1)} %maximum_bitcast_fusion), calls=%async_computation.1 | async-start | bytes 786432 | tf_op jit(solution)/shard_map/all_to_all | solution.py:153
  109.4 12.5 %all-to-all-start.2 = ((bf16[16,48,72]{2,1,0:T(8,128)(2,1)}), bf16[16,48,72]{2,1,0:T(8,128)(2,1)S(1)}, u32[]{:S(2)}, u32[]{:S(2)}) async-start(bf16[16,48,72]{2,1,0:T(8,128)(2,1)} %bitcast.10), calls=%async_computation.2 | async-start | bytes 393216 | tf_op jit(solution)/shard_map/all_to_all | solution.py:166
where the time goes:
time: 124 us; the launch traced here: 123 us
  blocking collectives  63 us (51%)
  waiting for transfers between devices  24.3 us (20%)
  matrix products  11 us (9%)
  starting transfers between devices  10.6 us (9%)
  other arithmetic  6.94 us (6%)
  local copies, waits for them, and re-layouts  6.71 us (5%)
    psum x1, blocking collectives, per_device(): modulation = lax.psum(partial_mod, 'patch')  63 us
    all_to_all x1, waiting for transfers between devices, per_device(): lax.all_to_all(pair_send, 'patch', split_axis=0, concat_axis=0, tiled=True)  12 us
    all_to_all x1, waiting for transfers between devices, per_device(): lax.all_to_all(head_result, 'patch', split_axis=0, concat_axis=0, tiled=T...  7.68 us
    all_to_all x1, waiting for transfers between devices, per_device(): lax.all_to_all(query_send, 'patch', split_axis=0, concat_axis=0, tiled=True)  4.69 us
    dot_general x1, matrix products, per_device(): jnp.dot(modulated, qkv_weight, preferred_element_type=jnp.float32)  4.6 us
    all_to_all x1, starting transfers between devices, per_device(): lax.all_to_all(pair_send, 'patch', split_axis=0, concat_axis=0, tiled=True)  3.55 us
    all_to_all x1, starting transfers between devices, per_device(): lax.all_to_all(query_send, 'patch', split_axis=0, concat_axis=0, tiled=True)  3.52 us
    all_to_all x1, starting transfers between devices, per_device(): lax.all_to_all(head_result, 'patch', split_axis=0, concat_axis=0, tiled=T...  3.52 us
  transfers between devices with their start and end apart: 3, of which 3 were waited for; matrix products, arithmetic and copies ran while one was open for 5% of the time, Pallas kernels for 0%

commit v1 on v0

--- a/solution.py
+++ b/solution.py
@@ -102,6 +102,18 @@
         .reshape(query_rows, head_count * head_size)
         .astype(jnp.bfloat16)
     )
+
+
+def butterfly_sum(value, axis):
+    devices = lax.axis_size(axis)
+    if devices & (devices - 1):
+        return lax.psum(value, axis)
+    step = 1
+    while step < devices:
+        pairs = [(index, index ^ step) for index in range(devices)]
+        value = value + lax.ppermute(value, axis, pairs)
+        step *= 2
+    return value
 
 
 def per_device(
@@ -121,7 +133,7 @@
     cond_part = jnp.dot(hidden_time, time_out, preferred_element_type=jnp.float32)
     activated = jax.nn.silu(cond_part).astype(jnp.bfloat16)
     partial_mod = jnp.dot(activated, ada_weight, preferred_element_type=jnp.float32)
-    modulation = lax.psum(partial_mod, "patch")
+    modulation = butterfly_sum(partial_mod, "patch")
     shift_mod = modulation[:, :model_width]
     scale_mod = modulation[:, model_width : 2 * model_width]
     gate_mod = modulation[:, 2 * model_width :]

time: 124 us -> 76.2 us (0.61)
  blocking collectives: 63 us -> 0 us
  starting transfers between devices: 10.6 us -> 21.7 us
  waiting for transfers between devices: 24.3 us -> 29.2 us
    psum x1 -> x0, blocking collectives: 63 us -> none  [per_device(): modulation = lax.psum(partial_mod, 'patch')]
    ppermute x0 -> x4, starting transfers between devices: none -> 8.36 us  [butterfly_sum(): value = value + lax.ppermute(value, axis, pairs)]
    ppermute x0 -> x4, waiting for transfers between devices: none -> 4.87 us  [butterfly_sum(): value = value + lax.ppermute(value, axis, pairs)]
    all_to_all x1, starting transfers between devices: 3.52 us -> 6.27 us  [per_device(): lax.all_to_all(query_send, 'patch', split_axis=0, concat_axis=0, tiled=True)]
  transfers between devices with their start and end apart: 3 -> 7, of which waited for: 3 -> 6; matrix products, arithmetic and copies ran while one was open for 5% -> 11% of each run, Pallas kernels for 0% -> 0%
where the time goes in v1:
time: 76.2 us; the launch traced here: 75.6 us
  waiting for transfers between devices  29.2 us (38%)
  starting transfers between devices  21.7 us (28%)
  matrix products  11 us (14%)
  local copies, waits for them, and re-layouts  6.71 us (9%)
  other arithmetic  5.98 us (8%)
  between operations  1.03 us (1%)
    all_to_all x1, waiting for transfers between devices, per_device(): lax.all_to_all(pair_send, 'patch', split_axis=0, concat_axis=0, tiled=True)  12 us
    ppermute x4, starting transfers between devices, butterfly_sum(): value = value + lax.ppermute(value, axis, pairs)  8.36 us
    all_to_all x1, waiting for transfers between devices, per_device(): lax.all_to_all(head_result, 'patch', split_axis=0, concat_axis=0, tiled=T...  7.68 us
    all_to_all x1, starting transfers between devices, per_device(): lax.all_to_all(query_send, 'patch', split_axis=0, concat_axis=0, tiled=True)  6.27 us
    ppermute x4, waiting for transfers between devices, butterfly_sum(): value = value + lax.ppermute(value, axis, pairs)  4.87 us
    all_to_all x1, waiting for transfers between devices, per_device(): lax.all_to_all(query_send, 'patch', split_axis=0, concat_axis=0, tiled=True)  4.73 us
    dot_general x1, matrix products, per_device(): jnp.dot(modulated, qkv_weight, preferred_element_type=jnp.float32)  4.6 us
    all_to_all x1, starting transfers between devices, per_device(): lax.all_to_all(pair_send, 'patch', split_axis=0, concat_axis=0, tiled=True)  3.55 us
  transfers between devices with their start and end apart: 7, of which 6 were waited for; matrix products, arithmetic and copies ran while one was open for 11% of the time, Pallas kernels for 0%

profile of v1, /device:TPU:0, one launch (start us, length us, event | category | flops | bytes accessed | tf_op | source)
XLA Modules:
  0.0 75.6 jit_solution(18222996981879237451)
XLA Ops:
  0.9 1.3 %convolution_reduce_fusion = f32[1152]{0:T(1024)S(1)} fusion(bf16[256,1]{0,1:T(2,128)(2,1)S(1)} %reshape.180, bf16[256,1152]{1,0:T(8,128)(2,1)} %param.13), kind=kOutput, calls=%fused_computation.11 | convolution fusion | flops 589824 | bytes 594944 | tf_op jit(solution)/shard_map/dot_general | solution.py:131
  2.2 1.6 %fusion.24 = f32[1,3456]{1,0:T(1,128)S(1)} fusion(bf16[72,3456]{1,0:T(8,128)(2,1)} %param.15, bf16[1152,1]{0,1:T(2,128)(2,1)S(1)} %reshape.182, bf16[1152,72]{0,1:T(8,128)(2,1)} %param.14), kind=kOutput, calls=%fused_computation.43 | convolution fusion | flops 663912 | bytes 679680 | tf_op jit(solution)/shard_map/dot_general | solution.py:135
  3.8 0.5 collective-permute-start
  4.3 0.8 %convert_bitcast_fusion = (f32[48]{0:T(128)S(1)}, f32[48]{0:T(128)S(1)}) fusion(s32[2,48]{1,0:T(2,128)} %param.10), kind=kLoop, calls=%fused_computation.52 | loop fusion | flops 96 | bytes 768 | tf_op jit(solution)/shard_map/convert_element_type | solution.py:26
  5.1 0.6 multiply_cosine_fusion
  5.8 1.0 %fusion.22 = f32[48]{0:T(128)S(1)} fusion(f32[48,1152]{1,0:T(8,128)S(1)} %concatenate.13, bf16[48,1152]{1,0:T(8,128)(2,1)} %param.9), kind=kLoop, calls=%fused_computation.30 | loop fusion | flops 165840 | bytes 331968 | tf_op jit(solution)/shard_map/reduce_sum | solution.py:141
  6.9 2.6 %collective-permute-start.1 = (f32[1,3456]{1,0:T(1,128)S(1)}, f32[1,3456]{1,0:T(1,128)S(1)}, u32[]{:S(2)}, u32[]{:S(2)}) collective-permute-start(f32[1,3456]{1,0:T(1,128)S(1)} %add.73), channel_id=1, source_target_pairs={{0,2},{1,3},{2,0},{3,1},{4,6},{5,7},{6,4},{7,5},{8,10},{9,11},{10,... | collective-permute-start | bytes 41480 | tf_op jit(solution)/shard_map/ppermute | solution.py:114
  9.4 1.7 %collective-permute-done.1 = f32[1,3456]{1,0:T(1,128)S(1)} collective-permute-done((f32[1,3456]{1,0:T(1,128)S(1)}, f32[1,3456]{1,0:T(1,128)S(1)}, u32[]{:S(2)}, u32[]{:S(2)}) %collective-permute-start.1) | collective-permute-done | bytes 13856 | tf_op jit(solution)/shard_map/ppermute | solution.py:114
  11.1 2.2 %collective-permute-start.2 = (f32[1,3456]{1,0:T(1,128)S(1)}, f32[1,3456]{1,0:T(1,128)S(1)}, u32[]{:S(2)}, u32[]{:S(2)}) collective-permute-start(f32[1,3456]{1,0:T(1,128)S(1)} %add.74), channel_id=1, source_target_pairs={{0,4},{1,5},{2,6},{3,7},{4,0},{5,1},{6,2},{7,3},{8,12},{9,13},{10,... | collective-permute-start | bytes 41480 | tf_op jit(solution)/shard_map/ppermute | solution.py:114
  13.5 1.5 %collective-permute-done.2 = f32[1,3456]{1,0:T(1,128)S(1)} collective-permute-done((f32[1,3456]{1,0:T(1,128)S(1)}, f32[1,3456]{1,0:T(1,128)S(1)}, u32[]{:S(2)}, u32[]{:S(2)}) %collective-permute-start.2) | collective-permute-done | bytes 13856 | tf_op jit(solution)/shard_map/ppermute | solution.py:114
  15.0 3.1 %collective-permute-start.3 = (f32[1,3456]{1,0:T(1,128)S(1)}, f32[1,3456]{1,0:T(1,128)S(1)}, u32[]{:S(2)}, u32[]{:S(2)}) collective-permute-start(f32[1,3456]{1,0:T(1,128)S(1)} %add.75), channel_id=1, source_target_pairs={{0,8},{1,9},{2,10},{3,11},{4,12},{5,13},{6,14},{7,15},{8,0},{9,1},... | collective-permute-start | bytes 41480 | tf_op jit(solution)/shard_map/ppermute | solution.py:114
  18.1 1.7 %collective-permute-done.3 = f32[1,3456]{1,0:T(1,128)S(1)} collective-permute-done((f32[1,3456]{1,0:T(1,128)S(1)}, f32[1,3456]{1,0:T(1,128)S(1)}, u32[]{:S(2)}, u32[]{:S(2)}) %collective-permute-start.3) | collective-permute-done | bytes 13856 | tf_op jit(solution)/shard_map/ppermute | solution.py:114
  19.9 4.6 %convolution_convert_fusion = bf16[48,3456]{1,0:T(8,128)(2,1)S(1)} fusion(bf16[1152,3456]{1,0:T(8,128)(2,1)} %param.16, f32[1152]{0:T(1024)S(1)} %get-tuple-element.6, f32[1152]{0:T(1024)S(1)} %get-tuple-element.7, f32[48]{0:T(128)S(1)} %add_rsqrt_fusion, f32[48]{0:T(128)S(1)} %broadcast_multiply_fusion, f32[48,1152]{1,0:T(8,128)S(1)} %concatenate.13, ...), kind=kOutput, calls=%fused_computation | convolution fusion | flops 382758912 | bytes 8635776 | tf_op jit(solution)/shard_map/dot_general | solution.py:149
  24.5 0.7 fusion.35
  25.5 0.7 copy.16
  26.2 6.3 %all-to-all-start = ((bf16[16,48,72]{2,1,0:T(8,128)(2,1)}), bf16[16,48,72]{2,1,0:T(8,128)(2,1)S(1)}, u32[]{:S(2)}, u32[]{:S(2)}) async-start(bf16[16,48,72]{2,1,0:T(8,128)(2,1)} %bitcast.38), calls=%async_computation | async-start | bytes 393216 | tf_op jit(solution)/shard_map/all_to_all | solution.py:164
  32.5 1.2 %reshape.175 = bf16[48,16,72]{2,1,0:T(8,128)(2,1)S(1)} reshape(bf16[48,1152]{1,0:T(8,128)(2,1)} %get-tuple-element.8) | data formatting | bytes 221184 | tf_op jit(solution)/shard_map/reshape | solution.py:156
  33.8 0.7 copy.11
  34.9 1.8 %maximum_bitcast_fusion = bf16[16,48,144]{2,1,0:T(8,128)(2,1)} fusion(bf16[48,16,72]{2,0,1:T(8,128)(2,1)S(1)} %copy.12, bf16[48,16,72]{2,0,1:T(8,128)(2,1)} %copy.11), kind=kLoop, calls=%fused_computation.13 | loop fusion | flops 442368 | bytes 442368 | tf_op jit(solution)/shard_map/transpose | solution.py:160
  36.8 4.7 %all-to-all-done = bf16[16,48,72]{2,1,0:T(8,128)(2,1)S(1)} async-done(((bf16[16,48,72]{2,1,0:T(8,128)(2,1)}), bf16[16,48,72]{2,1,0:T(8,128)(2,1)S(1)}, u32[]{:S(2)}, u32[]{:S(2)}) %all-to-all-start) | async-done | bytes 110624 | tf_op jit(solution)/shard_map/all_to_all | solution.py:164
  41.5 0.7 copy-done.2
  42.2 3.6 %all-to-all-start.1 = ((bf16[16,48,144]{2,1,0:T(8,128)(2,1)}), bf16[16,48,144]{2,1,0:T(8,128)(2,1)S(1)}, u32[]{:S(2)}, u32[]{:S(2)}) async-start(bf16[16,48,144]{2,1,0:T(8,128)(2,1)} %maximum_bitcast_fusion), calls=%async_computation.1 | async-start | bytes 786432 | tf_op jit(solution)/shard_map/all_to_all | solution.py:165
  45.9 12.0 %all-to-all-done.1 = bf16[16,48,144]{2,1,0:T(8,128)(2,1)S(1)} async-done(((bf16[16,48,144]{2,1,0:T(8,128)(2,1)}), bf16[16,48,144]{2,1,0:T(8,128)(2,1)S(1)}, u32[]{:S(2)}, u32[]{:S(2)}) %all-to-all-start.1) | async-done | bytes 221216 | tf_op jit(solution)/shard_map/all_to_all | solution.py:165
  57.9 1.5 %fusion = (f32[768]{0:T(1024)S(1)}, f32[768,768]{0,1:T(8,128)S(1)}) fusion(pred[768]{0:T(1024)(128)(4,1)S(1)} %lt.37, bf16[768,72]{1,0:T(8,128)(2,1)} %bitcast.41, bf16[768,144]{1,0:T(8,128)(2,1)S(1)} %bitcast.39), kind=kOutput, calls=%fused_computation.3 | convolution fusion | flops 86703360 | bytes 2670592 | tf_op jit(solution)/shard_map/qhd,khd->hqk/dot_general | solution.py:40
  59.3 0.6 fusion.1
  60.0 0.8 %fusion.12 = bf16[768,72]{0,1:T(8,128)(2,1)S(1)} fusion(f32[768,768]{0,1:T(8,128)S(1)} %get-tuple-element.22, f32[768]{0:T(1024)S(1)} %broadcast_maximum_fusion, pred[768]{0:T(1024)(128)(4,1)S(1)} %lt.37, bf16[768,144]{1,0:T(8,128)(2,1)S(1)} %bitcast.40, f32[768]{0:T(1024)S(1)} %get-tuple-element.12, f32[768]{0:T(1024)S(1)} %get-tuple-element.11), kind=kOutput, calls=%fused_computation.10 | convolution fusion | flops 88049664 | bytes 2679808 | tf_op jit(solution)/shard_map/hqk,khd->hqd/dot_general | solution.py:49
  60.8 0.8 %copy.13 = bf16[768,72]{1,0:T(8,128)(2,1)} copy(bf16[768,72]{0,1:T(8,128)(2,1)S(1)} %fusion.12) | data formatting | bytes 221184 | tf_op jit(solution)/shard_map/convert_element_type | solution.py:103
  61.6 3.5 %all-to-all-start.2 = ((bf16[16,48,72]{2,1,0:T(8,128)(2,1)}), bf16[16,48,72]{2,1,0:T(8,128)(2,1)S(1)}, u32[]{:S(2)}, u32[]{:S(2)}) async-start(bf16[16,48,72]{2,1,0:T(8,128)(2,1)} %bitcast.10), calls=%async_computation.2 | async-start | bytes 393216 | tf_op jit(solution)/shard_map/all_to_all | solution.py:178
  65.2 0.6 dynamic_slice.4
  65.7 0.6 compare_convert_fusion
  66.4 7.7 %all-to-all-done.2 = bf16[16,48,72]{2,1,0:T(8,128)(2,1)S(1)} async-done(((bf16[16,48,72]{2,1,0:T(8,128)(2,1)}), bf16[16,48,72]{2,1,0:T(8,128)(2,1)S(1)}, u32[]{:S(2)}, u32[]{:S(2)}) %all-to-all-start.2) | async-done | bytes 110624 | tf_op jit(solution)/shard_map/all_to_all | solution.py:178
  74.4 1.2 %add_convert_fusion = bf16[48,1152]{1,0:T(8,128)(2,1)} fusion(f32[48]{0:T(128)S(1)} %compare_convert_fusion, f32[1152]{0:T(1024)S(1)} %get-tuple-element.5, f32[48,1152]{1,0:T(8,128)S(1)} %concatenate.13, bf16[48,1152]{1,0:T(8,128)(2,1)S(1)} %copy-done.1, bf16[48,1152]{1,0:T(8,128)(2,1)S(1)} %reshape.179, bf16[1152,1152]{1,0:T(8,128)(2,1)S(1)} %copy-done), kind=kOutput, calls=%fused_computation.14 | convolution fusion | flops 127733760 | bytes 3211968 | tf_op jit(solution)/shard_map/dot_general | solution.py:183
  (32 shorter events, 1.8 us)
Async XLA Ops:
  0.0 74.4 %copy-start = (bf16[1152,1152]{1,0:T(8,128)(2,1)S(1)}, bf16[1152,1152]{1,0:T(8,128)(2,1)}, u32[]{:S(2)}) copy-start(bf16[1152,1152]{1,0:T(8,128)(2,1)} %param.17) | copy-start | bytes 7962628
  0.0 13.3 %copy-start.1 = (bf16[48,1152]{1,0:T(8,128)(2,1)S(1)}, bf16[48,1152]{1,0:T(8,128)(2,1)}, u32[]{:S(2)}) copy-start(bf16[48,1152]{1,0:T(8,128)(2,1)} %param.9) | copy-start | bytes 331780
  3.8 3.1 %collective-permute-start = (f32[1,3456]{1,0:T(1,128)S(1)}, f32[1,3456]{1,0:T(1,128)S(1)}, u32[]{:S(2)}, u32[]{:S(2)}) collective-permute-start(f32[1,3456]{1,0:T(1,128)S(1)} %fusion.24), channel_id=1, source_target_pairs={{0,1},{1,0},{2,3},{3,2},{4,5},{5,4},{6,7},{7,6},{8,9},{9,8},{10,11... | collective-permute-start | bytes 41480 | tf_op jit(solution)/shard_map/ppermute | solution.py:114
  6.9 4.2 %collective-permute-start.1 = (f32[1,3456]{1,0:T(1,128)S(1)}, f32[1,3456]{1,0:T(1,128)S(1)}, u32[]{:S(2)}, u32[]{:S(2)}) collective-permute-start(f32[1,3456]{1,0:T(1,128)S(1)} %add.73), channel_id=1, source_target_pairs={{0,2},{1,3},{2,0},{3,1},{4,6},{5,7},{6,4},{7,5},{8,10},{9,11},{10,... | collective-permute-start | bytes 41480 | tf_op jit(solution)/shard_map/ppermute | solution.py:114
  11.1 3.9 %collective-permute-start.2 = (f32[1,3456]{1,0:T(1,128)S(1)}, f32[1,3456]{1,0:T(1,128)S(1)}, u32[]{:S(2)}, u32[]{:S(2)}) collective-permute-start(f32[1,3456]{1,0:T(1,128)S(1)} %add.74), channel_id=1, source_target_pairs={{0,4},{1,5},{2,6},{3,7},{4,0},{5,1},{6,2},{7,3},{8,12},{9,13},{10,... | collective-permute-start | bytes 41480 | tf_op jit(solution)/shard_map/ppermute | solution.py:114
  15.0 4.8 %collective-permute-start.3 = (f32[1,3456]{1,0:T(1,128)S(1)}, f32[1,3456]{1,0:T(1,128)S(1)}, u32[]{:S(2)}, u32[]{:S(2)}) collective-permute-start(f32[1,3456]{1,0:T(1,128)S(1)} %add.75), channel_id=1, source_target_pairs={{0,8},{1,9},{2,10},{3,11},{4,12},{5,13},{6,14},{7,15},{8,0},{9,1},... | collective-permute-start | bytes 41480 | tf_op jit(solution)/shard_map/ppermute | solution.py:114
  24.5 21.2 %copy-start.3 = (s32[16]{0:T(128)S(1)}, s32[16]{0:T(128)}, u32[]{:S(2)}) copy-start(s32[16]{0:T(128)} %param.11) | copy-start | bytes 196
  26.2 15.2 %all-to-all-start = ((bf16[16,48,72]{2,1,0:T(8,128)(2,1)}), bf16[16,48,72]{2,1,0:T(8,128)(2,1)S(1)}, u32[]{:S(2)}, u32[]{:S(2)}) async-start(bf16[16,48,72]{2,1,0:T(8,128)(2,1)} %bitcast.38), calls=%async_computation | async-start | bytes 393216 | tf_op jit(solution)/shard_map/all_to_all | solution.py:164
  41.5 0.7 copy-start.2
  42.2 15.7 %all-to-all-start.1 = ((bf16[16,48,144]{2,1,0:T(8,128)(2,1)}), bf16[16,48,144]{2,1,0:T(8,128)(2,1)S(1)}, u32[]{:S(2)}, u32[]{:S(2)}) async-start(bf16[16,48,144]{2,1,0:T(8,128)(2,1)} %maximum_bitcast_fusion), calls=%async_computation.1 | async-start | bytes 786432 | tf_op jit(solution)/shard_map/all_to_all | solution.py:165
  61.6 12.5 %all-to-all-start.2 = ((bf16[16,48,72]{2,1,0:T(8,128)(2,1)}), bf16[16,48,72]{2,1,0:T(8,128)(2,1)S(1)}, u32[]{:S(2)}, u32[]{:S(2)}) async-start(bf16[16,48,72]{2,1,0:T(8,128)(2,1)} %bitcast.10), calls=%async_computation.2 | async-start | bytes 393216 | tf_op jit(solution)/shard_map/all_to_all | solution.py:178
